TPU v7x, 32 devices: a 4x4x1 block of a 4x4x8 slice. The times are simulated.
32 devices in a mesh: frag: 1 (over z), dev: 32 (over y, x, core).
Axes of the slice: x: 4, y: 4, z: 1, core: 2. Of those that a mesh axis runs over, the one named last changes fastest.
The devices are a block of a 4x4x8 slice.
Arguments:
- ao_ints: bfloat16 [160, 160, 160, 160], P(('frag', 'dev'))
- occ_coef: bfloat16 [160, 54], P('frag')
- virt_coef: bfloat16 [160, 64], P('frag')
Outputs:
- output: float32 [54, 64, 3456], P('frag', None, 'dev')
All inputs are finite; a program needn't handle non-finite values.
Results may differ from a plain program's by a relative error of at most 0.001.
Values are sent between devices in bfloat16 or wider.
A program may use at most 768 MiB of HBM per device.

v0:
```python
import jax
import jax.numpy as jnp
from jax import lax
from jax.sharding import PartitionSpec as P


def solution(mesh):
    def local_part(ao_rows, occ_coef, virt_coef):
        quarter = jnp.einsum("pqrs,rj->pqsj", ao_rows, occ_coef, preferred_element_type=jnp.float32).astype(jnp.bfloat16)
        half_ints = jnp.einsum("pqsj,sb->pqjb", quarter, virt_coef, preferred_element_type=jnp.float32).astype(jnp.bfloat16)
        rows_here, ao_dim, occ_dim, virt_dim = half_ints.shape
        half_ints = half_ints.reshape(rows_here, ao_dim, occ_dim * virt_dim)
        pair_block = lax.all_to_all(half_ints, "dev", 2, 0, tiled=True)
        three_quarter = jnp.einsum("qa,pqc->apc", virt_coef, pair_block, preferred_element_type=jnp.float32).astype(jnp.bfloat16)
        return jnp.einsum("pi,apc->iac", occ_coef, three_quarter, preferred_element_type=jnp.float32)

    return jax.shard_map(
        local_part,
        mesh=mesh,
        in_specs=(P(("frag", "dev"), None, None, None), P("frag", None), P("frag", None)),
        out_specs=P("frag", None, "dev"),
        check_vma=False,
    )
```

profile of v0, /device:TPU:97, one launch (start us, length us, event | category | flops | bytes accessed | tf_op | source)
XLA Modules:
  0.0 238.6 jit_solution(15945458596545014237)
XLA Ops:
  0.0 0.0 copy-start
  0.0 30.9 %convolution_convert_fusion = bf16[5,160,160,54]{2,3,1,0:T(8,128)(2,1)} fusion(bf16[5,160,160,160]{3,2,1,0:T(8,128)(2,1)} %param.3, bf16[160,54]{0,1:T(8,128)(2,1)} %param.4), kind=kOutput, calls=%fused_computation.2 | convolution fusion | flops 2218752000 | bytes 54801280 | tf_op jit(solution)/shard_map/pqrs,rj->pqsj/dot_general | solution.py:9
  30.9 0.0 copy-done
  30.9 24.2 %fusion.2 = bf16[5,160,54,64]{1,3,2,0:T(8,128)(2,1)} fusion(bf16[5,160,160,54]{2,3,1,0:T(8,128)(2,1)} %convolution_convert_fusion, bf16[160,64]{0,1:T(8,128)(2,1)S(1)} %copy-done), kind=kOutput, calls=%fused_computation.3 | convolution fusion | flops 887500800 | bytes 19374080 | tf_op jit(solution)/shard_map/pqsj,sb->pqjb/dot_general | solution.py:10
  55.2 26.2 %copy.27 = bf16[5,160,3456]{1,0,2:T(8,128)(2,1)} copy(bf16[5,160,3456]{1,2,0:T(8,128)(2,1)} %bitcast.35) | data formatting | bytes 11059200 | tf_op jit(solution)/shard_map/reshape | solution.py:12
  81.4 27.3 %reshape.8 = bf16[32,2,43200]{2,1,0:T(2,128)(2,1)} reshape(bf16[3456,5,160]{2,1,0:T(8,128)(2,1)} %bitcast.33) | data formatting | bytes 11059200
  108.6 78.5 %all_to_all.18 = bf16[32,2,43200]{2,1,0:T(2,128)(2,1)} all-to-all(bf16[32,2,43200]{2,1,0:T(2,128)(2,1)} %reshape.8), channel_id=1, replica_groups=mesh['frag'=1,'dev'=32] {'dev'}, dimensions={0} | all-to-all | bytes 11059200 | tf_op jit(solution)/shard_map/all_to_all | solution.py:13
  187.1 28.1 %reshape.9 = bf16[3456,5,160]{2,1,0:T(8,128)(2,1)} reshape(bf16[32,2,43200]{2,1,0:T(2,128)(2,1)} %all_to_all.18) | data formatting | bytes 11059200
  215.2 16.3 %copy.11 = bf16[32,5,160,108]{3,2,1,0:T(8,128)(2,1)} copy(bf16[32,5,160,108]{2,1,3,0:T(8,128)(2,1)} %bitcast.32) | data formatting | bytes 11059200 | tf_op jit(solution)/shard_map/all_to_all | solution.py:13
  231.5 0.0 copy-start.1
  231.5 3.9 %convert_bitcast_fusion = bf16[64,160,108]{2,0,1:T(8,128)(2,1)S(1)} fusion(bf16[160,160,108]{2,1,0:T(8,128)(2,1)} %bitcast.34, bf16[160,64]{0,1:T(8,128)(2,1)S(1)} %copy-done), kind=kOutput, calls=%fused_computation.6 | convolution fusion | flops 355000320 | bytes 7761920 | tf_op jit(solution)/shard_map/qa,pqc->apc/dot_general | solution.py:14
  235.4 0.0 copy-done.1
  235.4 1.7 fusion.7
  237.1 1.5 copy.13
Async XLA Ops:
  0.0 30.9 %copy-start = (bf16[160,64]{0,1:T(8,128)(2,1)S(1)}, bf16[160,64]{0,1:T(8,128)(2,1)}, u32[]{:S(2)}) copy-start(bf16[160,64]{0,1:T(8,128)(2,1)} %param.5) | copy-start | bytes 61444
  231.5 3.9 %copy-start.1 = (bf16[160,54]{0,1:T(8,128)(2,1)S(1)}, bf16[160,54]{0,1:T(8,128)(2,1)}, u32[]{:S(2)}) copy-start(bf16[160,54]{0,1:T(8,128)(2,1)} %param.4) | copy-start | bytes 51844
where the time goes:
time: 241 us; the launch traced here: 239 us
  local copies, waits for them, and re-layouts  99.3 us (41%)
  blocking collectives  78.5 us (33%)
  matrix products  60.7 us (25%)
    all_to_all x1, blocking collectives, local_part(): pair_block = lax.all_to_all(half_ints, 'dev', 2, 0, tiled=True)  78.5 us
    unnamed x6, local copies, waits for them, and re-layouts  55.4 us
    dot_general x1, matrix products, local_part(): jnp.einsum('pqrs,rj->pqsj', ao_rows, occ_coef, preferred_element_type=jnp...  30.9 us
    reshape x1, local copies, waits for them, and re-layouts, local_part(): half_ints = half_ints.reshape(rows_here, ao_dim, occ_dim * virt_dim)  26.2 us
    dot_general x1, matrix products, local_part(): jnp.einsum('pqsj,sb->pqjb', quarter, virt_coef, preferred_element_type=jn...  24.2 us
    all_to_all x1, local copies, waits for them, and re-layouts, local_part(): pair_block = lax.all_to_all(half_ints, 'dev', 2, 0, tiled=True)  16.3 us

commit v1 on v0

v1 whole, which is shorter than its diff:
```python
import functools

import jax
import jax.numpy as jnp
from jax import lax
from jax.experimental import pallas as pl
from jax.experimental.pallas import tpu as pltpu
from jax.sharding import PartitionSpec as P

MESH = pl.DeviceIdType.MESH
F32 = jnp.float32
BF16 = jnp.bfloat16
LANES = 128
CHUNK = 16
GROUP = 4
SLOTS = 8
SUB = 16


def dot(a, b):
    return jnp.dot(a, b, preferred_element_type=F32)


def dot_t(a, b):
    return lax.dot_general(a, b, (((1,), (1,)), ((), ())), preferred_element_type=F32)


def iota(shape, dim):
    return lax.broadcasted_iota(jnp.int32, shape, dim)


def one_hot(condition):
    return jnp.where(condition, 1.0, 0.0).astype(BF16)


def kernel(n, ao, co_t, cv_t, out, a_buf, h_buf, g_buf, s_buf, r_buf, kron, co_eo, cv_dup, a_sem, s_sem, r_sem):
    rows, ao_dim = ao.shape[0], ao.shape[1]
    occ, virt = co_t.shape[0], cv_t.shape[0]
    block = out.shape[2]
    half = 32
    pairs = occ // 2
    stride = h_buf.shape[0] // half
    chunks = ao_dim // CHUNK
    me = lax.axis_index("dev")
    barrier = pltpu.get_barrier_semaphore()

    def load(index):
        slot = lax.rem(index, SLOTS)
        return pltpu.make_async_copy(
            ao.at[index // chunks, pl.ds(lax.rem(index, chunks) * CHUNK, CHUNK)], a_buf.at[slot], a_sem.at[slot]
        )

    for index in range(SLOTS):
        load(jnp.int32(index)).start()

    @pl.loop(1, n)
    def _(k):
        pl.semaphore_signal(barrier, inc=1, device_id={"dev": lax.rem(me + k, n)}, device_id_type=MESH)

    row, col = iota((2 * half, occ), 0), iota((2 * half, occ), 1)
    want = jnp.where(row < half, 2 * row, 2 * (row - half) + 1)
    co_eo[...] = dot(one_hot(want == col), co_t[...]).astype(BF16)
    row, col = iota((2 * virt, virt), 0), iota((2 * virt, virt), 1)
    dup_t = dot(one_hot(lax.rem(row, virt) == col), cv_t[...]).astype(BF16)
    row, col = iota((ao_dim, ao_dim), 0), iota((ao_dim, ao_dim), 1)
    cv_dup[...] = dot_t(one_hot(row == col), dup_t).astype(BF16)

    lane = iota((half, LANES), 1)
    lane_v = iota((virt, LANES), 1)

    def row_step(p, carry):
        def chunk_step(ch, carry):
            index = p * chunks + ch
            slot = lax.rem(index, SLOTS)
            load(index).wait()
            for group in range(CHUNK // GROUP):
                quarter = [
                    dot(co_eo[...], a_buf[slot, group * GROUP + u]).astype(BF16) for u in range(GROUP)
                ]
                h = dot(jnp.concatenate(quarter, axis=0), cv_dup[...])
                for u in range(GROUP):
                    even = h[u * 2 * half : u * 2 * half + half]
                    odd = h[u * 2 * half + half : (u + 1) * 2 * half]
                    h_buf[pl.ds(ch * CHUNK + group * GROUP + u, half, stride=stride), :] = jnp.where(
                        lane < virt, even, odd
                    )

            @pl.when(index + SLOTS < rows * chunks)
            def _():
                load(index + SLOTS).start()

            return carry

        lax.fori_loop(0, chunks, chunk_step, 0)

        for first in range(0, pairs, 2):
            width = min(2, pairs - first)
            half_ints = jnp.concatenate(
                [h_buf[(first + w) * stride : (first + w) * stride + ao_dim, :].astype(BF16) for w in range(width)],
                axis=1,
            )
            g_buf[:, first * LANES : (first + width) * LANES] = dot(cv_t[...], half_ints)
        for d in range(n):
            start, offset = divmod(block * d, LANES)
            piece = g_buf[:, start * LANES : (start + 1) * LANES]
            if offset:
                piece = pltpu.roll(piece, LANES - offset, 1)
                if offset + block > LANES:
                    more = pltpu.roll(g_buf[:, (start + 1) * LANES : (start + 2) * LANES], LANES - offset, 1)
                    piece = jnp.where(lane_v < LANES - offset, piece, more)
            s_buf[p, d] = piece.astype(BF16)

        @pl.when(p == 0)
        def _():
            pl.semaphore_wait(barrier, n - 1)

        r_buf[p, me] = s_buf[p, me]

        @pl.loop(1, n)
        def _(k):
            to = lax.rem(me + k, n)
            pltpu.make_async_remote_copy(
                src_ref=s_buf.at[p, to],
                dst_ref=r_buf.at[p, me],
                send_sem=s_sem.at[p],
                recv_sem=r_sem.at[p],
                device_id={"dev": to},
                device_id_type=MESH,
            ).start()

        return carry

    lax.fori_loop(0, rows, row_step, 0)

    m, k = occ * SUB, n * SUB
    row, col = iota((m, occ), 0), iota((m, occ), 1)
    wide = dot(one_hot(row // SUB == col), co_t[...]).astype(BF16)
    same = lax.rem(iota((m, k), 0), SUB) == lax.rem(iota((m, k), 1), SUB)
    for p in range(rows):
        row, col = iota((ao_dim, k), 0), iota((ao_dim, k), 1)
        spread = dot(wide, one_hot((col // SUB) * rows + p == row))
        kron[p] = jnp.where(same, spread, 0.0).astype(BF16)

    def last(p, add):
        arrived = r_buf.at[p, pl.ds(0, n - 1)]
        pltpu.make_async_copy(arrived, arrived, r_sem.at[p]).wait()
        for first in range(0, virt // SUB, 2):
            three_quarter = jnp.concatenate(
                [
                    r_buf[p, :, (first + w) * SUB : (first + w + 1) * SUB, :].reshape(n * SUB, LANES)
                    for w in range(2)
                ],
                axis=1,
            )
            v = dot(kron[p], three_quarter)
            for w in range(2):
                a = (first + w) * SUB
                part = v[:, w * LANES : (w + 1) * LANES].reshape(occ, SUB, LANES)[:, :, :block]
                if add:
                    part = part + out[:, a : a + SUB, :]
                out[:, a : a + SUB, :] = part

    last(0, False)
    for p in range(1, rows):
        last(p, True)
    for p in range(rows):
        sent = s_buf.at[p, pl.ds(0, n - 1)]
        pltpu.make_async_copy(sent, sent, s_sem.at[p]).wait()


def solution(mesh):
    n = mesh.shape["dev"]

    def local_part(ao_rows, occ_coef, virt_coef):
        rows, ao_dim = ao_rows.shape[0], ao_rows.shape[1]
        occ, virt = occ_coef.shape[1], virt_coef.shape[1]
        block = occ * virt // n
        stride = ao_dim + 8
        vmem = pl.BlockSpec(memory_space=pltpu.VMEM)
        return pl.pallas_call(
            functools.partial(kernel, n),
            out_shape=jax.ShapeDtypeStruct((occ, virt, block), F32),
            in_specs=[pl.BlockSpec(memory_space=pl.ANY), vmem, vmem],
            out_specs=vmem,
            scratch_shapes=[
                pltpu.VMEM((SLOTS, CHUNK, ao_dim, ao_dim), BF16),
                pltpu.VMEM((32 * stride, LANES), F32),
                pltpu.VMEM((virt, (occ * virt // LANES) * LANES), F32),
                pltpu.VMEM((rows, n, virt, LANES), BF16),
                pltpu.VMEM((rows, n, virt, LANES), BF16),
                pltpu.VMEM((rows, occ * SUB, n * SUB), BF16),
                pltpu.VMEM((64, ao_dim), BF16),
                pltpu.VMEM((ao_dim, 2 * virt), BF16),
                pltpu.SemaphoreType.DMA((SLOTS,)),
                pltpu.SemaphoreType.DMA((rows,)),
                pltpu.SemaphoreType.DMA((rows,)),
            ],
            compiler_params=pltpu.CompilerParams(
                collective_id=0, has_side_effects=True, vmem_limit_bytes=56 * 1024 * 1024
            ),
            name="transform",
        )(ao_rows, occ_coef.T, virt_coef.T)

    return jax.shard_map(
        local_part,
        mesh=mesh,
        in_specs=(P(("frag", "dev"), None, None, None), P("frag", None), P("frag", None)),
        out_specs=P("frag", None, "dev"),
        check_vma=False,
    )
```

time: 241 us -> 66.2 us (0.27)
  local copies, waits for them, and re-layouts: 99.3 us -> 2.89 us
  blocking collectives: 78.5 us -> 0 us
  Pallas kernels: 0 us -> 63.2 us
  matrix products: 60.7 us -> 0 us
    all_to_all x1 -> x0, blocking collectives: 78.5 us -> none  [local_part(): pair_block = lax.all_to_all(half_ints, 'dev', 2, 0, tiled=True)]
    pallas_call x0 -> x1, Pallas kernels: none -> 63.2 us  [local_part(): pl.pallas_call(functools.partial(kernel, n), out_shape=jax.ShapeDtypeStru...]
    dot_general x4 -> x0, matrix products: 60.7 us -> none  [the longest x1 30.9 us: local_part(): jnp.einsum('pqrs,rj->pqsj', ao_rows, occ_coef, preferred_element_type=jnp...]
    unnamed x6 -> x1, local copies, waits for them, and re-layouts: 55.4 us -> 2.89 us
    reshape x1 -> x0, local copies, waits for them, and re-layouts: 26.2 us -> none  [local_part(): half_ints = half_ints.reshape(rows_here, ao_dim, occ_dim * virt_dim)]
    all_to_all x1 -> x0, local copies, waits for them, and re-layouts: 16.3 us -> none  [local_part(): pair_block = lax.all_to_all(half_ints, 'dev', 2, 0, tiled=True)]
where the time goes in v1:
time: 66.2 us; the launch traced here: 66.1 us
  Pallas kernels  63.2 us (95%)
  local copies, waits for them, and re-layouts  2.89 us (4%)
    pallas_call x1, Pallas kernels, local_part(): pl.pallas_call(functools.partial(kernel, n), out_shape=jax.ShapeDtypeStru...  63.2 us
    unnamed x1, local copies, waits for them, and re-layouts  2.89 us

profile of v1, /device:TPU:97, one launch (start us, length us, event | category | flops | bytes accessed | tf_op | source)
XLA Modules:
  0.0 66.1 jit_solution(6775461509268524244)
XLA Ops:
  0.0 63.2 %transform.1 = f32[54,64,108]{2,1,0:T(8,128)} custom-call(bf16[5,160,160,160]{3,2,1,0:T(8,128)(2,1)} %ao.1, bf16[54,160]{1,0:T(8,128)(2,1)} %bitcast.3, bf16[64,160]{1,0:T(8,128)(2,1)} %bitcast.2), custom_call_target="tpu_custom_call" | custom-call | tf_op jit(solution)/shard_map/transform/pallas_call | solution.py:180
  63.2 2.9 %copy.5 = f32[54,64,108]{2,1,0:T(8,128)} copy(f32[54,64,108]{2,1,0:T(8,128)} %transform.1) | data formatting | bytes 2985984

commit v2 on v1

v2 whole, which is shorter than its diff:
```python
import functools

import jax
import jax.numpy as jnp
from jax import lax
from jax.experimental import pallas as pl
from jax.experimental.pallas import tpu as pltpu
from jax.sharding import PartitionSpec as P

MESH = pl.DeviceIdType.MESH
F32 = jnp.float32
BF16 = jnp.bfloat16
LANES = 128
SUB = 8
CHUNK = 16
GROUP = 4
SLOTS = 8
HALF = 32


def dot(a, b):
    return jnp.dot(a, b, preferred_element_type=F32)


def dot_t(a, b):
    return lax.dot_general(a, b, (((1,), (1,)), ((), ())), preferred_element_type=F32)


def iota(shape, dim):
    return lax.broadcasted_iota(jnp.int32, shape, dim)


def one_hot(condition):
    return jnp.where(condition, 1.0, 0.0).astype(BF16)


def fold_plan(block):
    count = -(-block // (LANES - block))
    assert block % count == 0
    return count, block // count


def kernel(
    n, ao, co_in, cv_in, out, co_t, cv_t, a_buf, t_buf, h_buf, g_buf, s_buf, r_buf, acc, kron, co_eo, cv_dup,
    c_sem, a_sem, s_sem, r_sem,
):
    rows, ao_dim = ao.shape[0], ao.shape[1]
    occ, virt = co_in.shape[0], cv_in.shape[0]
    block = out.shape[2]
    count, width = fold_plan(block)
    kept = virt - SUB
    pairs = occ // 2
    stride = h_buf.shape[0] // HALF
    chunks = ao_dim // CHUNK
    me = lax.axis_index("dev")
    barrier = pltpu.get_barrier_semaphore()

    coef = [pltpu.make_async_copy(co_in, co_t, c_sem.at[0]), pltpu.make_async_copy(cv_in, cv_t, c_sem.at[1])]
    for copy in coef:
        copy.start()

    def load(index):
        slot = lax.rem(index, SLOTS)
        return pltpu.make_async_copy(
            ao.at[index // chunks, pl.ds(lax.rem(index, chunks) * CHUNK, CHUNK)], a_buf.at[slot], a_sem.at[slot]
        )

    for index in range(SLOTS):
        load(jnp.int32(index)).start()

    @pl.loop(1, n)
    def _(k):
        pl.semaphore_signal(barrier, inc=1, device_id={"dev": lax.rem(me + k, n)}, device_id_type=MESH)

    for copy in coef:
        copy.wait()
    row, col = iota((2 * HALF, occ), 0), iota((2 * HALF, occ), 1)
    want = jnp.where(row < HALF, 2 * row, 2 * (row - HALF) + 1)
    co_eo[...] = dot(one_hot(want == col), co_t[...]).astype(BF16)
    row, col = iota((2 * virt, virt), 0), iota((2 * virt, virt), 1)
    dup_t = dot(one_hot(lax.rem(row, virt) == col), cv_t[...]).astype(BF16)
    row, col = iota((ao_dim, ao_dim), 0), iota((ao_dim, ao_dim), 1)
    cv_dup[...] = dot_t(one_hot(row == col), dup_t).astype(BF16)

    lane = iota((HALF, LANES), 1)
    lane_v = iota((virt, LANES), 1)
    lane_s = iota((SUB, LANES), 1)

    def quarter_step(index):
        slot = lax.rem(index, SLOTS)
        load(index).wait()
        for u in range(CHUNK):
            t_buf[u * 2 * HALF : (u + 1) * 2 * HALF, :] = dot(co_eo[...], a_buf[slot, u]).astype(BF16)

        @pl.when(index + SLOTS < rows * chunks)
        def _():
            load(index + SLOTS).start()

    def half_step(ch):
        for group in range(CHUNK // GROUP):
            h = dot(t_buf[group * GROUP * 2 * HALF : (group + 1) * GROUP * 2 * HALF, :], cv_dup[...])
            for u in range(GROUP):
                even = h[u * 2 * HALF : u * 2 * HALF + HALF]
                odd = h[u * 2 * HALF + HALF : (u + 1) * 2 * HALF]
                h_buf[pl.ds(ch * CHUNK + group * GROUP + u, HALF, stride=stride), :] = jnp.where(
                    lane < virt, even, odd
                )

    def row_step(p, carry):
        def chunk_step(ch, carry):
            half_step(ch - 1)
            quarter_step(p * chunks + ch)
            return carry

        quarter_step(p * chunks)
        lax.fori_loop(1, chunks, chunk_step, 0)
        half_step(chunks - 1)

        for first in range(0, pairs, 2):
            many = min(2, pairs - first)
            half_ints = jnp.concatenate(
                [h_buf[(first + w) * stride : (first + w) * stride + ao_dim, :].astype(BF16) for w in range(many)],
                axis=1,
            )
            g_buf[:, first * LANES : (first + many) * LANES] = dot(cv_t[...], half_ints)
        for d in range(n):
            start, offset = divmod(block * d, LANES)
            piece = g_buf[:, start * LANES : (start + 1) * LANES]
            if offset:
                piece = pltpu.roll(piece, LANES - offset, 1)
                if offset + block > LANES:
                    more = pltpu.roll(g_buf[:, (start + 1) * LANES : (start + 2) * LANES], LANES - offset, 1)
                    piece = jnp.where(lane_v < LANES - offset, piece, more)
            top = piece[kept:]
            packed = []
            for g in range(kept // SUB):
                part = piece[g * SUB : (g + 1) * SUB]
                if g < count:
                    part = jnp.where(lane_s < block, part, pltpu.roll(top, block - g * width, 1))
                packed.append(part)
            s_buf[p, d] = jnp.concatenate(packed, axis=0).astype(BF16)

        @pl.when(p == 0)
        def _():
            pl.semaphore_wait(barrier, n - 1)

        r_buf[p, me] = s_buf[p, me]

        for k in range(1, n):
            to = lax.rem(me + k, n)
            pltpu.make_async_remote_copy(
                src_ref=s_buf.at[p, to],
                dst_ref=r_buf.at[p, me],
                send_sem=s_sem.at[p],
                recv_sem=r_sem.at[p],
                device_id={"dev": to},
                device_id_type=MESH,
            ).start()

        return carry

    lax.fori_loop(0, rows, row_step, 0)

    m, k = occ * SUB, n * SUB
    row, col = iota((m, occ), 0), iota((m, occ), 1)
    wide = dot(one_hot(row // SUB == col), co_t[...]).astype(BF16)
    same = lax.rem(iota((m, k), 0), SUB) == lax.rem(iota((m, k), 1), SUB)
    for p in range(rows):
        row, col = iota((ao_dim, k), 0), iota((ao_dim, k), 1)
        spread = dot(wide, one_hot((col // SUB) * rows + p == row))
        kron[p] = jnp.where(same, spread, 0.0).astype(BF16)

    for p in range(rows):
        arrived = r_buf.at[p, pl.ds(0, n - 1)]
        pltpu.make_async_copy(arrived, arrived, r_sem.at[p]).wait()
        for first in range(0, kept // SUB, 2):
            many = min(2, kept // SUB - first)
            three_quarter = jnp.concatenate(
                [
                    r_buf[p, :, (first + w) * SUB : (first + w + 1) * SUB, :].reshape(n * SUB, LANES)
                    for w in range(many)
                ],
                axis=1,
            )
            v = dot(kron[p], three_quarter)
            for w in range(many):
                g = first + w
                part = v[:, w * LANES : (w + 1) * LANES]
                if p:
                    part = part + acc[g]
                if p < rows - 1 or g < count:
                    acc[g] = part
                if p == rows - 1:
                    out[:, g * SUB : (g + 1) * SUB, :] = part.reshape(occ, SUB, LANES)[:, :, :block]
    lane_m = iota((m, LANES), 1)
    top = pltpu.roll(acc[0], LANES - block, 1)
    for g in range(1, count):
        top = jnp.where(lane_m < g * width, top, pltpu.roll(acc[g], (g * width + LANES - block) % LANES, 1))
    out[:, kept:, :] = top.reshape(occ, SUB, LANES)[:, :, :block]

    for p in range(rows):
        sent = s_buf.at[p, pl.ds(0, n - 1)]
        pltpu.make_async_copy(sent, sent, s_sem.at[p]).wait()


def solution(mesh):
    n = mesh.shape["dev"]

    def local_part(ao_rows, occ_coef, virt_coef):
        rows, ao_dim = ao_rows.shape[0], ao_rows.shape[1]
        occ, virt = occ_coef.shape[1], virt_coef.shape[1]
        block = occ * virt // n
        kept = virt - SUB
        stride = ao_dim + 8
        hbm = pl.BlockSpec(memory_space=pltpu.HBM)
        return pl.pallas_call(
            functools.partial(kernel, n),
            out_shape=pltpu.VMEM((occ, virt, block), F32),
            in_specs=[hbm, hbm, hbm],
            out_specs=pl.BlockSpec(memory_space=pltpu.VMEM),
            scratch_shapes=[
                pltpu.VMEM((occ, ao_dim), BF16),
                pltpu.VMEM((virt, ao_dim), BF16),
                pltpu.VMEM((SLOTS, CHUNK, ao_dim, ao_dim), BF16),
                pltpu.VMEM((CHUNK * 2 * HALF, ao_dim), BF16),
                pltpu.VMEM((HALF * stride, LANES), F32),
                pltpu.VMEM((virt, occ * virt), F32),
                pltpu.VMEM((rows, n, kept, LANES), BF16),
                pltpu.VMEM((rows, n, kept, LANES), BF16),
                pltpu.VMEM((kept // SUB, occ * SUB, LANES), F32),
                pltpu.VMEM((rows, occ * SUB, n * SUB), BF16),
                pltpu.VMEM((2 * HALF, ao_dim), BF16),
                pltpu.VMEM((ao_dim, 2 * virt), BF16),
                pltpu.SemaphoreType.DMA((2,)),
                pltpu.SemaphoreType.DMA((SLOTS,)),
                pltpu.SemaphoreType.DMA((rows,)),
                pltpu.SemaphoreType.DMA((rows,)),
            ],
            compiler_params=pltpu.CompilerParams(
                collective_id=0, has_side_effects=True, vmem_limit_bytes=50 * 1024 * 1024
            ),
            name="transform",
        )(ao_rows, *[pltpu.with_memory_space_constraint(c, pltpu.HBM) for c in (occ_coef.T, virt_coef.T)])

    return jax.shard_map(
        local_part,
        mesh=mesh,
        in_specs=(P(("frag", "dev"), None, None, None), P("frag", None), P("frag", None)),
        out_specs=P("frag", None, "dev"),
        check_vma=False,
    )
```

time: 66.2 us -> 56 us (0.85)
  Pallas kernels: 63.2 us -> 54.7 us
  local copies, waits for them, and re-layouts: 2.89 us -> 1.21 us
    pallas_call x1, Pallas kernels: 63.2 us -> 54.7 us  [local_part(): pl.pallas_call(functools.partial(kernel, n), out_shape=pltpu.VMEM((occ, v...]
    unnamed x1, local copies, waits for them, and re-layouts: 2.89 us -> 1.21 us
where the time goes in v2:
time: 56 us; the launch traced here: 55.9 us
  Pallas kernels  54.7 us (98%)
  local copies, waits for them, and re-layouts  1.21 us (2%)
    pallas_call x1, Pallas kernels, local_part(): pl.pallas_call(functools.partial(kernel, n), out_shape=pltpu.VMEM((occ, v...  54.7 us
    unnamed x1, local copies, waits for them, and re-layouts  1.21 us

profile of v2, /device:TPU:97, one launch (start us, length us, event | category | flops | bytes accessed | tf_op | source)
XLA Modules:
  0.0 55.9 jit_solution(7462265154921294965)
XLA Ops:
  0.0 54.7 %transform.1 = f32[54,64,108]{2,1,0:T(8,128)S(1)} custom-call(bf16[5,160,160,160]{3,2,1,0:T(8,128)(2,1)} %ao.1, bf16[54,160]{1,0:T(8,128)(2,1)} %bitcast.3, bf16[64,160]{1,0:T(8,128)(2,1)} %bitcast.2), custom_call_target="tpu_custom_call" | custom-call | tf_op jit(solution)/shard_map/transform/pallas_call | solution.py:216
  54.7 1.2 %copy.5 = f32[54,64,108]{2,1,0:T(8,128)} copy(f32[54,64,108]{2,1,0:T(8,128)S(1)} %transform.1) | data formatting | bytes 2985984

commit v3 on v2

--- a/solution.py
+++ b/solution.py
@@ -14,7 +14,7 @@
 SUB = 8
 CHUNK = 16
 GROUP = 4
-SLOTS = 8
+SLOTS = 4
 HALF = 32
 
 

time: 56 us -> 54.2 us (0.968)
  Pallas kernels: 54.7 us -> 52.9 us
    pallas_call x1, Pallas kernels: 54.7 us -> 52.9 us  [local_part(): pl.pallas_call(functools.partial(kernel, n), out_shape=pltpu.VMEM((occ, v...]
where the time goes in v3:
time: 54.2 us; the launch traced here: 54.1 us
  Pallas kernels  52.9 us (98%)
  local copies, waits for them, and re-layouts  1.21 us (2%)
    pallas_call x1, Pallas kernels, local_part(): pl.pallas_call(functools.partial(kernel, n), out_shape=pltpu.VMEM((occ, v...  52.9 us
    unnamed x1, local copies, waits for them, and re-layouts  1.21 us

profile of v3, /device:TPU:97, one launch (start us, length us, event | category | flops | bytes accessed | tf_op | source)
XLA Modules:
  0.0 54.1 jit_solution(16166719231748439921)
XLA Ops:
  0.0 52.9 %transform.1 = f32[54,64,108]{2,1,0:T(8,128)S(1)} custom-call(bf16[5,160,160,160]{3,2,1,0:T(8,128)(2,1)} %ao.1, bf16[54,160]{1,0:T(8,128)(2,1)} %bitcast.3, bf16[64,160]{1,0:T(8,128)(2,1)} %bitcast.2), custom_call_target="tpu_custom_call" | custom-call | tf_op jit(solution)/shard_map/transform/pallas_call | solution.py:216
  52.9 1.2 %copy.5 = f32[54,64,108]{2,1,0:T(8,128)} copy(f32[54,64,108]{2,1,0:T(8,128)S(1)} %transform.1) | data formatting | bytes 2985984

commit v4 on v3

--- a/solution.py
+++ b/solution.py
@@ -12,9 +12,9 @@
 BF16 = jnp.bfloat16
 LANES = 128
 SUB = 8
-CHUNK = 16
+CHUNK = 32
 GROUP = 4
-SLOTS = 4
+SLOTS = 3
 HALF = 32
 
 
@@ -211,7 +211,7 @@
         occ, virt = occ_coef.shape[1], virt_coef.shape[1]
         block = occ * virt // n
         kept = virt - SUB
-        stride = ao_dim + 8
+        stride = ao_dim + 4
         hbm = pl.BlockSpec(memory_space=pltpu.HBM)
         return pl.pallas_call(
             functools.partial(kernel, n),

time: 54.2 us -> 47 us (0.87)
  Pallas kernels: 52.9 us -> 45.7 us
    pallas_call x1, Pallas kernels: 52.9 us -> 45.7 us  [local_part(): pl.pallas_call(functools.partial(kernel, n), out_shape=pltpu.VMEM((occ, v...]
where the time goes in v4:
time: 47 us; the launch traced here: 46.9 us
  Pallas kernels  45.7 us (97%)
  local copies, waits for them, and re-layouts  1.21 us (3%)
    pallas_call x1, Pallas kernels, local_part(): pl.pallas_call(functools.partial(kernel, n), out_shape=pltpu.VMEM((occ, v...  45.7 us
    unnamed x1, local copies, waits for them, and re-layouts  1.21 us

profile of v4, /device:TPU:97, one launch (start us, length us, event | category | flops | bytes accessed | tf_op | source)
XLA Modules:
  0.0 46.9 jit_solution(6406908771176089860)
XLA Ops:
  0.0 45.7 %transform.1 = f32[54,64,108]{2,1,0:T(8,128)S(1)} custom-call(bf16[5,160,160,160]{3,2,1,0:T(8,128)(2,1)} %ao.1, bf16[54,160]{1,0:T(8,128)(2,1)} %bitcast.3, bf16[64,160]{1,0:T(8,128)(2,1)} %bitcast.2), custom_call_target="tpu_custom_call" | custom-call | tf_op jit(solution)/shard_map/transform/pallas_call | solution.py:216
  45.7 1.2 %copy.5 = f32[54,64,108]{2,1,0:T(8,128)} copy(f32[54,64,108]{2,1,0:T(8,128)S(1)} %transform.1) | data formatting | bytes 2985984
